TPU v7x, 32 devices: a whole 2x2x4 slice. The times are simulated.
32 devices in a mesh: rep: 4 (over x, core), shard: 8 (over z, y).
Axes of the slice: x: 2, y: 2, z: 4, core: 2. Of those that a mesh axis runs over, the one named last changes fastest.
Arguments:
- outer_delta: float32 [4, 2097152], P('rep', 'shard'), may hold values from -40 to 40
- offsets: int32 [65], replicated, may hold values from 0 to 2097152, as said below
- parameters: float32 [2097152], P('shard'), may hold values from -6 to 6
- momentum: float32 [2097152], P(('shard', 'rep')), may hold values from -1.2 to 1.2
Outputs:
- new_parameters: float32 [2097152], P('shard')
- new_momentum: float32 [2097152], P(('shard', 'rep'))
Inputs may be any that keep to these rules, and one draw needn't show every extreme that they name: `offsets`: strictly increasing multiples of 128, the first 0 and the last 2097152.
All inputs are finite; a program needn't handle non-finite values.
Results may differ from a plain program's by a relative error of at most 0.0003.
Values sent between devices are 32-bit elements; how exact they have to be, the bound alone decides.
A program may use at most 64 MiB of HBM per device.

v0:
```python
import math

import jax
import jax.numpy as jnp
from jax import lax
from jax.sharding import PartitionSpec as P

LR_OUTER = 0.7
MU_OUTER = 0.9
CLIP_RMS = 0.1
EPSILON = 1e-06


def one_hot_rows(first_pos, block_len, offsets):
    tensors = offsets.shape[0] - 1
    positions = first_pos + jnp.arange(block_len, dtype=jnp.int32)
    segment = jnp.sum((positions[:, None] >= offsets[None, 1:tensors]).astype(jnp.int32), axis=1)
    return (segment[:, None] == jnp.arange(tensors, dtype=jnp.int32)[None, :]).astype(jnp.float32)


def tensor_squares(values, first_pos, offsets):
    total_len = values.shape[0]
    block_len = math.gcd(total_len, 8192)
    value_rows = values.reshape(total_len // block_len, block_len)
    block_starts = first_pos + jnp.arange(total_len // block_len, dtype=jnp.int32) * block_len

    def partial_squares(items):
        row_values, row_start = items
        selector = one_hot_rows(row_start, block_len, offsets)
        return jnp.dot(
            row_values * row_values,
            selector,
            precision=lax.Precision.HIGHEST,
            preferred_element_type=jnp.float32,
        )

    return jnp.sum(lax.map(partial_squares, (value_rows, block_starts)), axis=0)


def element_factor(factor, total_len, first_pos, offsets):
    block_len = math.gcd(total_len, 8192)
    block_starts = first_pos + jnp.arange(total_len // block_len, dtype=jnp.int32) * block_len

    def spread_factor(row_start):
        selector = one_hot_rows(row_start, block_len, offsets)
        return jnp.dot(
            selector, factor, precision=lax.Precision.HIGHEST, preferred_element_type=jnp.float32
        )

    return lax.map(spread_factor, block_starts).reshape(total_len)


def clip_factor(squares_sum, offsets):
    lengths = (offsets[1:] - offsets[:-1]).astype(jnp.float32)
    return jnp.minimum(1.0, CLIP_RMS * jnp.sqrt(lengths) * lax.rsqrt(squares_sum + EPSILON))


def on_device(outer_delta, offsets, parameters, momentum):
    replicas = lax.axis_size("rep")
    shard_len = parameters.shape[0]
    own_len = shard_len // replicas
    rep_index = lax.axis_index("rep")
    shard_start = lax.axis_index("shard") * shard_len
    local_delta = outer_delta.reshape(shard_len)
    avg_delta = lax.psum_scatter(local_delta, "rep", scatter_dimension=0, tiled=True) / jnp.float32(
        replicas
    )
    first_pos = shard_start + rep_index * own_len
    squares_sum = lax.psum(tensor_squares(avg_delta, first_pos, offsets), ("shard", "rep"))
    factor = clip_factor(squares_sum, offsets)
    scaled = avg_delta * element_factor(factor, own_len, first_pos, offsets)
    owned_params = lax.dynamic_slice_in_dim(parameters, rep_index * own_len, own_len)
    new_momentum = MU_OUTER * momentum + scaled
    new_owned = owned_params - LR_OUTER * (scaled + MU_OUTER * new_momentum)
    new_parameters = lax.all_gather(new_owned, "rep", axis=0, tiled=True)
    return (new_parameters, new_momentum)


def solution(mesh):
    return jax.shard_map(
        on_device,
        mesh=mesh,
        in_specs=(P("rep", "shard"), P(), P("shard"), P(("shard", "rep"))),
        out_specs=(P("shard"), P(("shard", "rep"))),
        check_vma=False,
    )
```

profile of v0, /device:TPU:0, one launch (start us, length us, event | category | flops | bytes accessed | tf_op | source)
XLA Modules:
  0.0 162.3 jit_solution(8617485549905927681)
XLA Ops:
  7.2 0.7 all-reduce.3.cloned.1.call-update
  8.0 0.7 dynamic-slice
  9.4 40.0 %all-reduce.3.cloned.1.call-done = f32[262144]{0:T(1024)} async-done(((f32[262144]{0:T(1024)}), f32[262144]{0:T(1024)}) %all-reduce.3.cloned.1.call-update) | async-done | bytes 1048592
  49.4 1.0 dynamic-slice_multiply_fusion
  50.4 23.2 %while.20 = (s32[]{:T(128)}, f32[8,64]{1,0:T(8,128)S(1)}, f32[8,8192]{1,0:T(8,128)S(1)}, s32[8]{0:T(128)S(1)}, s32[65]{0:T(128)S(1)}, /*index=5*/s32[]{:T(128)}, s32[]{:T(128)}) while((s32[]{:T(128)}, f32[8,64]{1,0:T(8,128)S(1)}, f32[8,8192]{1,0:T(8,128)S(1)}, s32[8]{0:T(128)S(1)}, s32[65]{0:T(128)S(1)}, /*index=5*/s32[]{:T(128)}, ...), condition=%wide.region_3.4_spmd, body=%wide.region_1.3_spmd.sunk | while | flops 8372226 | bytes 165465 | solution.py:37
  50.5 0.7 dynamic_slice.24
  51.1 0.7 iota_add_fusion.4
  52.2 1.1 fusion.10
  53.4 0.7 dynamic_slice.24
  54.0 0.7 iota_add_fusion.4
  54.8 0.3 convert_reduce_fusion.4
  55.1 1.1 fusion.10
  56.3 0.7 dynamic_slice.24
  56.9 0.7 iota_add_fusion.4
  57.7 0.3 convert_reduce_fusion.4
  58.0 1.1 fusion.10
  59.2 0.7 dynamic_slice.24
  59.8 0.7 iota_add_fusion.4
  60.6 0.3 convert_reduce_fusion.4
  60.9 1.1 fusion.10
  62.1 0.7 dynamic_slice.24
  62.7 0.7 iota_add_fusion.4
  63.5 0.3 convert_reduce_fusion.4
  63.8 1.1 fusion.10
  65.0 0.7 dynamic_slice.24
  65.6 0.7 iota_add_fusion.4
  66.4 0.3 convert_reduce_fusion.4
  66.8 1.1 fusion.10
  67.9 0.7 dynamic_slice.24
  68.5 0.7 iota_add_fusion.4
  69.7 1.1 fusion.10
  70.8 0.7 dynamic_slice.24
  71.4 0.7 iota_add_fusion.4
  72.6 1.1 fusion.10
  73.7 39.8 %psum.7 = f32[64]{0:T(128)S(1)} all-reduce(f32[64]{0:T(128)S(1)} %reduce_sum.27), channel_id=1, replica_groups=mesh['rep'=4,'shard'=8] {'shard','rep'}, use_global_device_ids=true, to_apply=%region_5.6 | all-reduce | flops 64 | bytes 512 | tf_op jit(solution)/shard_map/psum | solution.py:69
  113.6 20.5 %while.21 = (s32[]{:T(128)}, f32[8,8192]{1,0:T(8,128)S(1)}, s32[8]{0:T(128)S(1)}, s32[65]{0:T(128)S(1)}, f32[64]{0:T(128)S(1)}, /*index=5*/s32[]{:T(128)}, s32[]{:T(128)}) while((s32[]{:T(128)}, f32[8,8192]{1,0:T(8,128)S(1)}, s32[8]{0:T(128)S(1)}, s32[65]{0:T(128)S(1)}, f32[64]{0:T(128)S(1)}, /*index=5*/s32[]{:T(128)}, s32[]{:T(128)}) %tuple.50), condition=%wide.region_8.9_spmd, body=%wide.region_6.8_spmd.sunk | while | flops 8364034 | bytes 230485 | solution.py:50
  113.6 0.6 dynamic_slice.25
  114.2 0.6 iota_add_fusion.5
  114.9 0.3 convert_reduce_fusion.5
  115.2 0.7 fusion.12
  116.1 0.6 dynamic_slice.25
  116.7 0.6 iota_add_fusion.5
  117.8 0.7 fusion.12
  118.7 0.6 dynamic_slice.25
  119.3 0.6 iota_add_fusion.5
  120.4 0.7 fusion.12
  121.3 0.6 dynamic_slice.25
  121.9 0.6 iota_add_fusion.5
  122.9 0.7 fusion.12
  123.9 0.6 dynamic_slice.25
  124.4 0.6 iota_add_fusion.5
  125.5 0.7 fusion.12
  126.4 0.6 dynamic_slice.25
  127.0 0.6 iota_add_fusion.5
  128.1 0.7 fusion.12
  129.0 0.6 dynamic_slice.25
  129.6 0.6 iota_add_fusion.5
  130.6 0.7 fusion.12
  131.6 0.6 dynamic_slice.25
  132.1 0.6 iota_add_fusion.5
  133.2 0.7 fusion.12
  134.2 1.9 %multiply_subtract_fusion = (f32[65536]{0:T(1024)}, f32[65536]{0:T(1024)}) fusion(f32[262144]{0:T(1024)} %param.10, s32[]{:T(128)S(6)} %select_n.3, f32[65536]{0:T(1024)S(1)} %copy-done, f32[65536]{0:T(1024)S(1)} %bitcast.24, f32[262144]{0:T(1024)} %all-reduce.3.cloned.1.call-done, u32[]{:T(128)S(6)} %multiply.2), kind=kLoop, calls=%fused_computation.15 | loop fusion | flops 524288 | bytes 1572872 | tf_op jit(solution)/shard_map/sub | solution.py:74
  136.1 17.0 %all-gather.2.cloned.1.call-done = f32[262144]{0:T(1024)} async-done(((f32[65536]{0:T(1024)}), f32[262144]{0:T(1024)}) %all-gather.2.cloned.1.call-update) | async-done | bytes 1048592 | tf_op jit(solution)/shard_map/all_gather | solution.py:75
  153.2 2.3 %copy.24 = f32[262144]{0:T(1024)} copy(f32[262144]{0:T(1024)} %all-gather.2.cloned.1.call-done) | data formatting | bytes 2097152
  (58 shorter events, 6.2 us)
Async XLA Ops:
  7.2 0.8 copy-start.2
  7.2 42.2 %all-reduce.3.cloned.1.call-start = ((), (), s32[]{:S(2)}) async-start(), calls=%async_computation.1 | async-start | bytes 2097152
  7.2 43.2 %copy-start.1 = (s32[65]{0:T(128)S(1)}, s32[65]{0:T(128)}, u32[]{:S(2)}) copy-start(s32[65]{0:T(128)} %param.9) | copy-start | bytes 784
  7.9 145.3 %all-gather.2.cloned.1.call-start = ((), (), s32[]{:S(2)}) async-start(), calls=%async_computation | async-start | bytes 1310720 | tf_op jit(solution)/shard_map/all_gather | solution.py:75
  113.6 20.6 %copy-start = (f32[65536]{0:T(1024)S(1)}, f32[65536]{0:T(1024)}, u32[]{:S(2)}) copy-start(f32[65536]{0:T(1024)} %param.11) | copy-start | bytes 786436
Sparse Core Ops, SparseCore 0:
  10.3 39.0 all-reduce.2
  136.3 16.8 all-gather.1
where the time goes:
time: 163 us; the launch traced here: 162 us
  waiting for transfers between devices  57.7 us (35%)
  blocking collectives  39.8 us (24%)
  other arithmetic  19.1 us (12%)
  local copies, waits for them, and re-layouts  15.6 us (10%)
  between operations  14.9 us (9%)
  matrix products  14.5 us (9%)
    unnamed x3, waiting for transfers between devices  40.7 us
    psum x1, blocking collectives, on_device(): lax.psum(tensor_squares(avg_delta, first_pos, offsets), ('shard', 'rep'))  39.8 us
    all_gather x1, waiting for transfers between devices, on_device(): new_parameters = lax.all_gather(new_owned, 'rep', axis=0, tiled=True)  17 us
    add x16, other arithmetic, one_hot_rows(): positions = first_pos + jnp.arange(block_len, dtype=jnp.int32)  10.7 us
    dynamic_slice x16, local copies, waits for them, and re-layouts, tensor_squares(): return jnp.sum(lax.map(partial_squares, (value_rows, block_starts)), axis=0)  10 us
    dot_general x8, matrix products, partial_squares(): jnp.dot(row_values * row_values, selector, precision=lax.Precision.HIGHES...  8.58 us
    dot_general x8, matrix products, spread_factor(): jnp.dot(selector, factor, precision=lax.Precision.HIGHEST, preferred_elem...  5.97 us
    reduce_sum x16, other arithmetic, one_hot_rows(): jnp.sum((positions[:, None] >= offsets[None, 1:tensors]).astype(jnp.int32...  5.37 us
  transfers between devices with their start and end apart: 2, of which 2 were waited for; matrix products, arithmetic and copies ran while one was open for 0% of the time, Pallas kernels for 0%

commit v1 on v0

v1 whole, which is shorter than its diff:
```python
import functools

import jax
import jax.numpy as jnp
from jax import lax
from jax.experimental import pallas as pl
from jax.experimental.pallas import tpu as pltpu
from jax.sharding import PartitionSpec as P

LR_OUTER = 0.7
MU_OUTER = 0.9
CLIP_RMS = 0.1
EPSILON = 1e-06
LANES = 128
MESH = pl.DeviceIdType.MESH


def split_dot(wide):
    high = wide.astype(jnp.bfloat16)
    low = (wide - high.astype(jnp.float32)).astype(jnp.bfloat16)
    both = jnp.concatenate([high, low], axis=1)
    ones = jnp.ones((2 * LANES, LANES), jnp.bfloat16)
    return jnp.dot(both, ones, preferred_element_type=jnp.float32)


def outer_step(
    replicas, shards, tensors, block, chunk,
    offsets, delta_in, params_in, momentum_in,
    full, new_momentum,
    delta, params, momentum, from_twin, chip_sum, from_chips, average, partial, partials,
    load_sem, twin_send, twin_recv, chip_send, chip_recv, norm_send, norm_recv,
    out_send, out_recv, own_send, own_recv, pass_send, pass_recv,
):
    chips = replicas // 2
    pieces = block // chunk
    devices = replicas * shards
    rep = lax.axis_index("rep")
    shard = lax.axis_index("shard")
    me = rep * shards + shard
    chip = lax.div(rep, 2)
    core = lax.rem(rep, 2)
    twin = (rep + 1) - 2 * core

    def chip_at(step):
        return lax.rem(chip + step, chips)

    def part(piece):
        return pl.ds(piece * chunk, chunk)

    own_rows = pl.ds(pl.multiple_of(rep * block, 8), block)
    loads = [
        pltpu.make_async_copy(delta_in, delta, load_sem.at[0]),
        pltpu.make_async_copy(params_in.at[own_rows], params, load_sem.at[1]),
        pltpu.make_async_copy(momentum_in, momentum, load_sem.at[2]),
    ]
    for load in loads:
        load.start()

    barrier = pltpu.get_barrier_semaphore()

    def greet(step, carry):
        other = lax.rem(me + step, devices)
        pl.semaphore_signal(
            barrier, inc=1, device_id=(lax.div(other, shards), lax.rem(other, shards)),
            device_id_type=MESH,
        )
        return carry

    lax.fori_loop(1, devices, greet, 0)

    lane = lax.broadcasted_iota(jnp.int32, (1, LANES), 1)
    first = jnp.zeros((1, LANES), jnp.int32)
    last = jnp.zeros((1, LANES), jnp.int32)
    for t in range(tensors):
        first = jnp.where(lane == t, offsets[t], first)
        last = jnp.where(lane == t, offsets[t + 1], last)

    loads[0].wait()
    pl.semaphore_wait(barrier, devices - 1)

    def block_rows(owner, piece):
        return pl.ds(pl.multiple_of(owner * block + piece * chunk, 8), chunk)

    steps = list(range(1, chips)) + [0]
    twin_copies = {}
    for step in steps:
        for piece in range(pieces):
            owner = 2 * chip_at(step) + (1 - core)
            copy = pltpu.make_async_remote_copy(
                src_ref=delta.at[block_rows(owner, piece)],
                dst_ref=from_twin.at[step, part(piece)],
                send_sem=twin_send.at[step, piece],
                recv_sem=twin_recv.at[step, piece],
                device_id=(twin, shard),
                device_id_type=MESH,
            )
            copy.start()
            twin_copies[step, piece] = copy

    chip_copies = {}
    for piece in range(pieces):
        for step in range(1, chips):
            owner = 2 * chip_at(step) + core
            twin_copies[step, piece].wait_recv()
            chip_sum[step - 1, part(piece)] = (
                delta[block_rows(owner, piece)] + from_twin[step, part(piece)]
            )
            copy = pltpu.make_async_remote_copy(
                src_ref=chip_sum.at[step - 1, part(piece)],
                dst_ref=from_chips.at[step - 1, part(piece)],
                send_sem=chip_send.at[step - 1, piece],
                recv_sem=chip_recv.at[step - 1, piece],
                device_id=(owner, shard),
                device_id_type=MESH,
            )
            copy.start()
            chip_copies[step, piece] = copy

    base = (shard * replicas + rep) * block

    def in_tensor(piece):
        row = lax.broadcasted_iota(jnp.int32, (chunk, LANES), 0)
        position = (row + (base + piece * chunk)) * LANES
        return (position >= first) & (position < last)

    squares = jnp.zeros((1, LANES), jnp.float32)
    for piece in range(pieces):
        twin_copies[0, piece].wait_recv()
        total = delta[block_rows(rep, piece)] + from_twin[0, part(piece)]
        for step in range(1, chips):
            chip_copies[step, piece].wait_recv()
            total = total + from_chips[step - 1, part(piece)]
        mean = total * jnp.float32(1.0 / replicas)
        average[part(piece)] = mean
        row_sums = split_dot(mean * mean)
        squares = squares + jnp.sum(
            jnp.where(in_tensor(piece), row_sums, 0.0), axis=0, keepdims=True
        )
    partial[...] = squares

    def tell(step, carry):
        other = lax.rem(me + step, devices)
        pltpu.make_async_remote_copy(
            src_ref=partial,
            dst_ref=partials.at[pl.ds(step - 1, 1)],
            send_sem=norm_send,
            recv_sem=norm_recv,
            device_id=(lax.div(other, shards), lax.rem(other, shards)),
            device_id_type=MESH,
        ).start()
        return carry

    lax.fori_loop(1, devices, tell, 0)
    loads[1].wait()
    loads[2].wait()
    pltpu.make_async_copy(partials, partials, norm_recv).wait()
    squares = squares + jnp.sum(partials[...], axis=0, keepdims=True)
    lengths = (last - first).astype(jnp.float32)
    factor = jnp.minimum(1.0, CLIP_RMS * jnp.sqrt(lengths) * lax.rsqrt(squares + EPSILON))

    out_copies = {}
    own_copies = {}
    for piece in range(pieces):
        spread = split_dot(jnp.where(in_tensor(piece), factor, 0.0))
        scaled = average[part(piece)] * spread
        moved = MU_OUTER * momentum[part(piece)] + scaled
        new_momentum[part(piece)] = moved
        mine = block_rows(rep, piece)
        full[mine] = params[part(piece)] - LR_OUTER * (scaled + MU_OUTER * moved)
        for step in range(1, chips):
            copy = pltpu.make_async_remote_copy(
                src_ref=full.at[mine],
                dst_ref=full.at[mine],
                send_sem=out_send.at[step - 1, piece],
                recv_sem=out_recv.at[step - 1, piece],
                device_id=(2 * chip_at(step) + core, shard),
                device_id_type=MESH,
            )
            copy.start()
            out_copies[step, piece] = copy
        copy = pltpu.make_async_remote_copy(
            src_ref=full.at[mine],
            dst_ref=full.at[mine],
            send_sem=own_send.at[piece],
            recv_sem=own_recv.at[piece],
            device_id=(twin, shard),
            device_id_type=MESH,
        )
        copy.start()
        own_copies[piece] = copy

    pass_copies = []
    for piece in range(pieces):
        for step in range(1, chips):
            sender = 2 * chip_at(chips - step) + core
            out_copies[step, piece].wait_recv()
            copy = pltpu.make_async_remote_copy(
                src_ref=full.at[block_rows(sender, piece)],
                dst_ref=full.at[block_rows(sender, piece)],
                send_sem=pass_send.at[step - 1, piece],
                recv_sem=pass_recv.at[step - 1, piece],
                device_id=(twin, shard),
                device_id_type=MESH,
            )
            copy.start()
            pass_copies.append(copy)

    for copy in twin_copies.values():
        copy.wait_send()
    for copy in chip_copies.values():
        copy.wait_send()
    pltpu.make_async_copy(partials, partials, norm_send).wait()
    for copy in out_copies.values():
        copy.wait_send()
    for copy in own_copies.values():
        copy.wait()
    for copy in pass_copies:
        copy.wait()


def on_device(replicas, shards, outer_delta, offsets, parameters, momentum):
    rows = parameters.shape[0] // LANES
    block = rows // replicas
    chips = replicas // 2
    chunk = min(block, 128)
    pieces = block // chunk
    devices = replicas * shards
    hbm = pl.BlockSpec(memory_space=pl.ANY)
    vmem = pl.BlockSpec(memory_space=pltpu.VMEM)
    dma = pltpu.SemaphoreType.DMA
    f32 = jnp.float32
    full, moved = pl.pallas_call(
        functools.partial(
            outer_step, replicas, shards, offsets.shape[0] - 1, block, chunk
        ),
        out_shape=(
            jax.ShapeDtypeStruct((rows, LANES), f32),
            jax.ShapeDtypeStruct((block, LANES), f32),
        ),
        in_specs=[pl.BlockSpec(memory_space=pltpu.SMEM), hbm, hbm, hbm],
        out_specs=(vmem, vmem),
        scratch_shapes=[
            pltpu.VMEM((rows, LANES), f32),
            pltpu.VMEM((block, LANES), f32),
            pltpu.VMEM((block, LANES), f32),
            pltpu.VMEM((chips, block, LANES), f32),
            pltpu.VMEM((chips - 1, block, LANES), f32),
            pltpu.VMEM((chips - 1, block, LANES), f32),
            pltpu.VMEM((block, LANES), f32),
            pltpu.VMEM((1, LANES), f32),
            pltpu.VMEM((devices - 1, LANES), f32),
            dma((3,)),
            dma((chips, pieces)),
            dma((chips, pieces)),
            dma((chips - 1, pieces)),
            dma((chips - 1, pieces)),
            dma,
            dma,
            dma((chips - 1, pieces)),
            dma((chips - 1, pieces)),
            dma((pieces,)),
            dma((pieces,)),
            dma((chips - 1, pieces)),
            dma((chips - 1, pieces)),
        ],
        compiler_params=pltpu.CompilerParams(collective_id=0, has_side_effects=True),
        name="outer_step",
    )(
        offsets,
        outer_delta.reshape(rows, LANES),
        parameters.reshape(rows, LANES),
        momentum.reshape(block, LANES),
    )
    return full.reshape(rows * LANES), moved.reshape(block * LANES)


def solution(mesh):
    return jax.shard_map(
        functools.partial(on_device, mesh.shape["rep"], mesh.shape["shard"]),
        mesh=mesh,
        in_specs=(P("rep", "shard"), P(), P("shard"), P(("shard", "rep"))),
        out_specs=(P("shard"), P(("shard", "rep"))),
        check_vma=False,
    )
```

time: 163 us -> 33.3 us (0.20)
  waiting for transfers between devices: 57.7 us -> 0 us
  blocking collectives: 39.8 us -> 0 us
  Pallas kernels: 0 us -> 29.5 us
  other arithmetic: 19.1 us -> 0 us
  matrix products: 14.5 us -> 0 us
  between operations: 14.9 us -> 0.65 us
  local copies, waits for them, and re-layouts: 15.6 us -> 3.03 us
    unnamed x3 -> x0, waiting for transfers between devices: 40.7 us -> none
    psum x1 -> x0, blocking collectives: 39.8 us -> none  [on_device(): lax.psum(tensor_squares(avg_delta, first_pos, offsets), ('shard', 'rep'))]
    pallas_call x0 -> x1, Pallas kernels: none -> 29.5 us  [on_device(): pl.pallas_call(functools.partial(outer_step, replicas, shards, offsets.sh...]
    all_gather x1 -> x0, waiting for transfers between devices: 17 us -> none  [on_device(): new_parameters = lax.all_gather(new_owned, 'rep', axis=0, tiled=True)]
    dot_general x16 -> x0, matrix products: 14.5 us -> none  [the longest x8 8.58 us: partial_squares(): jnp.dot(row_values * row_values, selector, precision=lax.Precision.HIGHES...]
    add x17 -> x0, other arithmetic: 10.8 us -> none  [the longest x16 10.7 us: one_hot_rows(): positions = first_pos + jnp.arange(block_len, dtype=jnp.int32)]
    dynamic_slice x16 -> x0, local copies, waits for them, and re-layouts: 10 us -> none  [tensor_squares(): return jnp.sum(lax.map(partial_squares, (value_rows, block_starts)), axis=0)]
    reduce_sum x17 -> x0, other arithmetic: 5.39 us -> none  [the longest x16 5.37 us: one_hot_rows(): jnp.sum((positions[:, None] >= offsets[None, 1:tensors]).astype(jnp.int32...]
  transfers between devices with their start and end apart: 2 -> 0, of which waited for: 2 -> 0; matrix products, arithmetic and copies ran while one was open for 0% -> 0% of each run, Pallas kernels for 0% -> 0%
where the time goes in v1:
time: 33.3 us; the launch traced here: 33.1 us
  Pallas kernels  29.5 us (89%)
  local copies, waits for them, and re-layouts  3.03 us (9%)
  between operations  0.65 us (2%)
    pallas_call x1, Pallas kernels, on_device(): pl.pallas_call(functools.partial(outer_step, replicas, shards, offsets.sh...  29.5 us
    unnamed x4, local copies, waits for them, and re-layouts  3.03 us

profile of v1, /device:TPU:0, one launch (start us, length us, event | category | flops | bytes accessed | tf_op | source)
XLA Modules:
  0.0 33.1 jit_solution(17634547465575439996)
XLA Ops:
  0.6 29.5 %outer_step.1 = (f32[2048,128]{1,0:T(8,128)}, f32[512,128]{1,0:T(8,128)}) custom-call(s32[65]{0:T(128)} %offsets.1, f32[2048,128]{1,0:T(8,128)} %bitcast.5, f32[2048,128]{1,0:T(8,128)} %bitcast.6, f32[512,128]{1,0:T(8,128)} %bitcast.8), custom_call_target="tpu_custom_call" | custom-call | tf_op jit(solution)/shard_map/outer_step/pallas_call | solution.py:232
  30.1 0.0 copy-start
  30.1 2.3 %copy.8 = f32[262144]{0:T(1024)} copy(f32[262144]{0:T(1024)} %bitcast.7) | data formatting | bytes 2097152
  32.4 0.0 copy-done
  32.4 0.7 %copy.9 = f32[65536]{0:T(1024)} copy(f32[65536]{0:T(1024)S(1)} %bitcast.9) | data formatting | bytes 524288
Async XLA Ops:
  30.1 2.3 %copy-start = (f32[512,128]{1,0:T(8,128)S(1)}, f32[512,128]{1,0:T(8,128)}, u32[]{:S(2)}) copy-start(f32[512,128]{1,0:T(8,128)} %get-tuple-element.5) | copy-start | bytes 786436

commit v2 on v1

--- a/solution.py
+++ b/solution.py
@@ -218,6 +218,17 @@
         copy.wait()
 
 
+def put_out(full, moved, full_out, moved_out, sem):
+    copies = [
+        pltpu.make_async_copy(full, full_out, sem.at[0]),
+        pltpu.make_async_copy(moved, moved_out, sem.at[1]),
+    ]
+    for copy in copies:
+        copy.start()
+    for copy in copies:
+        copy.wait()
+
+
 def on_device(replicas, shards, outer_delta, offsets, parameters, momentum):
     rows = parameters.shape[0] // LANES
     block = rows // replicas
@@ -225,7 +236,7 @@
     chunk = min(block, 128)
     pieces = block // chunk
     devices = replicas * shards
-    hbm = pl.BlockSpec(memory_space=pl.ANY)
+    hbm = pl.BlockSpec(memory_space=pltpu.HBM)
     vmem = pl.BlockSpec(memory_space=pltpu.VMEM)
     dma = pltpu.SemaphoreType.DMA
     f32 = jnp.float32
@@ -263,14 +274,26 @@
             dma((chips - 1, pieces)),
             dma((chips - 1, pieces)),
         ],
-        compiler_params=pltpu.CompilerParams(collective_id=0, has_side_effects=True),
+        compiler_params=pltpu.CompilerParams(collective_id=0, has_side_effects=True, vmem_limit_bytes=12 * 2**20),
         name="outer_step",
     )(
-        offsets,
-        outer_delta.reshape(rows, LANES),
-        parameters.reshape(rows, LANES),
-        momentum.reshape(block, LANES),
+        pltpu.with_memory_space_constraint(offsets, pltpu.HBM),
+        pltpu.with_memory_space_constraint(outer_delta.reshape(rows, LANES), pltpu.HBM),
+        pltpu.with_memory_space_constraint(parameters.reshape(rows, LANES), pltpu.HBM),
+        pltpu.with_memory_space_constraint(momentum.reshape(block, LANES), pltpu.HBM),
     )
+    full, moved = pl.pallas_call(
+        put_out,
+        out_shape=(
+            jax.ShapeDtypeStruct((rows, LANES), f32),
+            jax.ShapeDtypeStruct((block, LANES), f32),
+        ),
+        in_specs=[pl.BlockSpec(memory_space=pl.ANY)] * 2,
+        out_specs=(hbm, hbm),
+        scratch_shapes=[dma((2,))],
+        compiler_params=pltpu.CompilerParams(vmem_limit_bytes=2**20),
+        name="put_out",
+    )(full, moved)
     return full.reshape(rows * LANES), moved.reshape(block * LANES)
 
 

time: 33.3 us -> 30.2 us (0.907)
  local copies, waits for them, and re-layouts: 3.03 us -> 0 us
    unnamed x4 -> x0, local copies, waits for them, and re-layouts: 3.03 us -> none
    pallas_call x0 -> x1, Pallas kernels: none -> 1.07 us  [on_device(): pl.pallas_call(put_out, out_shape=(jax.ShapeDtypeStruct((rows, LANES), f3...]
    pallas_call x1, Pallas kernels: 29.5 us -> 28.4 us  [on_device(): pl.pallas_call(functools.partial(outer_step, replicas, shards, offsets.sh...]
where the time goes in v2:
time: 30.2 us; the launch traced here: 30.1 us
  Pallas kernels  29.5 us (98%)
  between operations  0.64 us (2%)
    pallas_call x1, Pallas kernels, on_device(): pl.pallas_call(functools.partial(outer_step, replicas, shards, offsets.sh...  28.4 us
    pallas_call x1, Pallas kernels, on_device(): pl.pallas_call(put_out, out_shape=(jax.ShapeDtypeStruct((rows, LANES), f3...  1.07 us

profile of v2, /device:TPU:0, one launch (start us, length us, event | category | flops | bytes accessed | tf_op | source)
XLA Modules:
  0.0 30.1 jit_solution(4480892533664070656)
XLA Ops:
  0.6 28.4 %outer_step.1 = (f32[2048,128]{1,0:T(8,128)S(1)}, f32[512,128]{1,0:T(8,128)S(1)}) custom-call(s32[65]{0:T(128)} %offsets.1, f32[2048,128]{1,0:T(8,128)} %bitcast.5, f32[2048,128]{1,0:T(8,128)} %bitcast.6, f32[512,128]{1,0:T(8,128)} %bitcast.7), custom_call_target="tpu_custom_call" | custom-call | tf_op jit(solution)/shard_map/outer_step/pallas_call | solution.py:243
  29.0 1.1 %put_out.1 = (f32[2048,128]{1,0:T(8,128)}, f32[512,128]{1,0:T(8,128)}) custom-call(f32[2048,128]{1,0:T(8,128)S(1)} %get-tuple-element.6.full, f32[512,128]{1,0:T(8,128)S(1)} %get-tuple-element.7.moved), custom_call_target="tpu_custom_call" | custom-call | tf_op jit(solution)/shard_map/put_out/pallas_call | solution.py:285

commit v3 on v2

v3 whole, which is shorter than its diff:
```python
import functools

import jax
import jax.numpy as jnp
from jax import lax
from jax.experimental import pallas as pl
from jax.experimental.pallas import tpu as pltpu
from jax.sharding import PartitionSpec as P

LR_OUTER = 0.7
MU_OUTER = 0.9
CLIP_RMS = 0.1
EPSILON = 1e-06
LANES = 128
MESH = pl.DeviceIdType.MESH


def split_dot(wide):
    high = wide.astype(jnp.bfloat16)
    low = (wide - high.astype(jnp.float32)).astype(jnp.bfloat16)
    both = jnp.concatenate([high, low], axis=1)
    ones = jnp.ones((2 * LANES, LANES), jnp.bfloat16)
    return jnp.dot(both, ones, preferred_element_type=jnp.float32)


def outer_step(
    replicas, shards, tensors, block, chunk, early, ahead, before,
    offsets, delta_in, params_in, momentum_in,
    full, new_momentum,
    delta, params, momentum, average, from_twin, chip_sum, from_chips, partial, partials,
    ready, everyone, load_sem, twin_send, twin_recv, chip_send, chip_recv, norm_send, norm_recv,
    out_send, out_recv, own_send, own_recv, pass_send, pass_recv,
):
    chips = replicas // 2
    pieces = block // chunk
    devices = replicas * shards
    rep = lax.axis_index("rep")
    shard = lax.axis_index("shard")
    me = rep * shards + shard
    chip = lax.div(rep, 2)
    core = lax.rem(rep, 2)
    twin = (rep + 1) - 2 * core
    peers = range(1, chips)

    def peer(step):
        return 2 * lax.rem(chip + step, chips) + core

    def part(piece):
        return pl.ds(piece * chunk, chunk)

    def block_rows(owner, piece):
        return pl.ds(pl.multiple_of(owner * block + piece * chunk, 8), chunk)

    def to(other, src, dst, send, recv):
        copy = pltpu.make_async_remote_copy(
            src_ref=src, dst_ref=dst, send_sem=send, recv_sem=recv,
            device_id=(other, shard), device_id_type=MESH,
        )
        copy.start()
        return copy

    own_rows = pl.ds(pl.multiple_of(rep * block, 8), block)
    loads = [
        pltpu.make_async_copy(momentum_in, momentum.at[own_rows], load_sem.at[0]),
        pltpu.make_async_copy(delta_in, delta, load_sem.at[1]),
        pltpu.make_async_copy(params_in, params, load_sem.at[2]),
    ]
    for load in loads:
        load.start()

    barrier = pltpu.get_barrier_semaphore()

    @pl.when(rep != 0)
    def _():
        for step in range(1, replicas):
            other = lax.rem(rep + step, replicas)

            @pl.when(other != 0)
            def _():
                pl.semaphore_signal(
                    barrier, inc=1, device_id=(other, shard), device_id_type=MESH
                )

        pl.semaphore_wait(barrier, replicas - 1)
        pl.semaphore_signal(ready, inc=1, device_id=(0, shard), device_id_type=MESH)

    @pl.when(rep == 0)
    def _():
        for other in range(1, replicas):
            pl.semaphore_signal(
                barrier, inc=1, device_id=(other, shard), device_id_type=MESH
            )
        pl.semaphore_wait(ready, replicas - 1)
        for step in range(1, shards):
            pl.semaphore_signal(
                barrier, inc=1, device_id=(rep, lax.rem(shard + step, shards)),
                device_id_type=MESH,
            )

    lane = lax.broadcasted_iota(jnp.int32, (1, LANES), 1)
    first = jnp.zeros((1, LANES), jnp.int32)
    last = jnp.zeros((1, LANES), jnp.int32)
    for t in range(tensors):
        first = jnp.where(lane == t, offsets[t], first)
        last = jnp.where(lane == t, offsets[t + 1], last)

    def in_tensor(owner, piece):
        row = lax.broadcasted_iota(jnp.int32, (chunk, LANES), 0)
        start = (shard * replicas + owner) * block + piece * chunk
        position = (row + start) * LANES
        return (position >= first) & (position < last)

    arrays = (momentum, average, full)
    sent = {}
    own = {}
    passed = []

    def share(kind, piece):
        mine = arrays[kind].at[block_rows(rep, piece)]
        for step in peers:
            sent[kind, step, piece] = to(
                peer(step), mine, mine,
                out_send.at[kind, step - 1, piece], out_recv.at[kind, step - 1, piece],
            )
        own[kind, piece] = to(
            twin, mine, mine, own_send.at[kind, piece], own_recv.at[kind, piece]
        )

    def pass_on(kind, piece):
        for step in peers:
            sent[kind, step, piece].wait_recv()
            rows = arrays[kind].at[block_rows(peer(chips - step), piece)]
            passed.append((kind, piece, to(
                twin, rows, rows,
                pass_send.at[kind, step - 1, piece], pass_recv.at[kind, step - 1, piece],
            )))

    loads[0].wait()
    loads[1].wait()

    twin_copies = {}
    for step in list(peers) + [0]:
        for piece in range(pieces):
            owner = peer(step) + 1 - 2 * core
            twin_copies[step, piece] = to(
                twin, delta.at[block_rows(owner, piece)], from_twin.at[step, part(piece)],
                twin_send.at[step, piece], twin_recv.at[step, piece],
            )
        if step == (1 if chips > 1 else 0):
            for piece in range(ahead):
                share(0, piece)

    chip_copies = {}
    for piece in range(pieces):
        for step in peers:
            twin_copies[step, piece].wait_recv()
            chip_sum[step - 1, part(piece)] = (
                delta[block_rows(peer(step), piece)] + from_twin[step, part(piece)]
            )
            chip_copies[step, piece] = to(
                peer(step), chip_sum.at[step - 1, part(piece)],
                from_chips.at[step - 1, part(piece)],
                chip_send.at[step - 1, piece], chip_recv.at[step - 1, piece],
            )
    if ahead < early:
        share(0, ahead)

    @pl.when(rep == 0)
    def _():
        pl.semaphore_wait(barrier, shards - 1)
        for other in range(1, replicas):
            pl.semaphore_signal(
                everyone, inc=1, device_id=(other, shard), device_id_type=MESH
            )

    squares = jnp.zeros((1, LANES), jnp.float32)
    for piece in range(pieces):
        twin_copies[0, piece].wait_recv()
        total = delta[block_rows(rep, piece)] + from_twin[0, part(piece)]
        for step in peers:
            chip_copies[step, piece].wait_recv()
            total = total + from_chips[step - 1, part(piece)]
        mean = total * jnp.float32(1.0 / replicas)
        average[block_rows(rep, piece)] = mean
        row_sums = split_dot(mean * mean)
        squares = squares + jnp.sum(
            jnp.where(in_tensor(rep, piece), row_sums, 0.0), axis=0, keepdims=True
        )
    partial[...] = squares

    @pl.when(rep != 0)
    def _():
        pl.semaphore_wait(everyone, 1)

    def tell(step, carry):
        other = lax.rem(me + step, devices)
        pltpu.make_async_remote_copy(
            src_ref=partial,
            dst_ref=partials.at[pl.ds(step - 1, 1)],
            send_sem=norm_send,
            recv_sem=norm_recv,
            device_id=(lax.div(other, shards), lax.rem(other, shards)),
            device_id_type=MESH,
        ).start()
        return carry

    lax.fori_loop(1, devices, tell, 0)

    queue = []
    for piece in range(early):
        share(1, piece)
        if (0, piece) not in own:
            share(0, piece)
        queue.append((1, piece))
        queue.append((0, piece))
    queue.sort(key=lambda item: not (item[0] == 0 and item[1] <= ahead))
    for kind, piece in queue[:before]:
        pass_on(kind, piece)

    loads[2].wait()
    pltpu.make_async_copy(partials, partials, norm_recv).wait()
    squares = squares + jnp.sum(partials[...], axis=0, keepdims=True)
    lengths = (last - first).astype(jnp.float32)
    factor = jnp.minimum(1.0, CLIP_RMS * jnp.sqrt(lengths) * lax.rsqrt(squares + EPSILON))

    def update(owner, piece):
        rows = block_rows(owner, piece)
        spread = split_dot(jnp.where(in_tensor(owner, piece), factor, 0.0))
        scaled = average[rows] * spread
        moved = MU_OUTER * momentum[rows] + scaled
        full[rows] = params[rows] - LR_OUTER * (scaled + MU_OUTER * moved)
        return moved

    for piece in range(early, pieces):
        new_momentum[part(piece)] = update(rep, piece)
        share(2, piece)
    for kind, piece in queue[before:]:
        pass_on(kind, piece)
    for piece in range(early):
        new_momentum[part(piece)] = update(rep, piece)
    for piece in range(early):
        own[0, piece].wait_recv()
        own[1, piece].wait_recv()
        update(twin, piece)
    for piece in range(early):
        for step in peers:
            update(peer(step), piece)
    for piece in range(early, pieces):
        pass_on(2, piece)
    for kind, piece, copy in passed:
        if kind < 2:
            copy.wait_recv()
    for piece in range(early):
        for step in peers:
            update(peer(step) + 1 - 2 * core, piece)

    for copy in (*twin_copies.values(), *chip_copies.values(), *sent.values()):
        copy.wait_send()
    pltpu.make_async_copy(partials, partials, norm_send).wait()
    for (kind, piece), copy in own.items():
        copy.wait_send()
        if kind == 2:
            copy.wait_recv()
    for kind, piece, copy in passed:
        copy.wait_send()
        if kind == 2:
            copy.wait_recv()


def put_out(full, moved, full_out, moved_out, sem):
    copies = [
        pltpu.make_async_copy(full, full_out, sem.at[0]),
        pltpu.make_async_copy(moved, moved_out, sem.at[1]),
    ]
    for copy in copies:
        copy.start()
    for copy in copies:
        copy.wait()


def on_device(replicas, shards, outer_delta, offsets, parameters, momentum):
    rows = parameters.shape[0] // LANES
    block = rows // replicas
    chips = replicas // 2
    chunk = min(block, 128)
    pieces = block // chunk
    early = pieces * 3 // 4
    ahead = min(early, 1)
    before = min(2 * early, 2)
    devices = replicas * shards
    hbm = pl.BlockSpec(memory_space=pltpu.HBM)
    vmem = pl.BlockSpec(memory_space=pltpu.VMEM)
    dma = pltpu.SemaphoreType.DMA
    f32 = jnp.float32
    full, moved = pl.pallas_call(
        functools.partial(
            outer_step, replicas, shards, offsets.shape[0] - 1, block, chunk,
            early, ahead, before,
        ),
        out_shape=(
            jax.ShapeDtypeStruct((rows, LANES), f32),
            jax.ShapeDtypeStruct((block, LANES), f32),
        ),
        in_specs=[pl.BlockSpec(memory_space=pltpu.SMEM), hbm, hbm, hbm],
        out_specs=(vmem, vmem),
        scratch_shapes=[
            pltpu.VMEM((rows, LANES), f32),
            pltpu.VMEM((rows, LANES), f32),
            pltpu.VMEM((rows, LANES), f32),
            pltpu.VMEM((rows, LANES), f32),
            pltpu.VMEM((chips, block, LANES), f32),
            pltpu.VMEM((chips - 1, block, LANES), f32),
            pltpu.VMEM((chips - 1, block, LANES), f32),
            pltpu.VMEM((1, LANES), f32),
            pltpu.VMEM((devices - 1, LANES), f32),
            pltpu.SemaphoreType.REGULAR,
            pltpu.SemaphoreType.REGULAR,
            dma((3,)),
            dma((chips, pieces)),
            dma((chips, pieces)),
            dma((chips - 1, pieces)),
            dma((chips - 1, pieces)),
            dma,
            dma,
            dma((3, chips - 1, pieces)),
            dma((3, chips - 1, pieces)),
            dma((3, pieces)),
            dma((3, pieces)),
            dma((3, chips - 1, pieces)),
            dma((3, chips - 1, pieces)),
        ],
        compiler_params=pltpu.CompilerParams(collective_id=0, has_side_effects=True, vmem_limit_bytes=12 * 2**20),
        name="outer_step",
    )(
        pltpu.with_memory_space_constraint(offsets, pltpu.HBM),
        pltpu.with_memory_space_constraint(outer_delta.reshape(rows, LANES), pltpu.HBM),
        pltpu.with_memory_space_constraint(parameters.reshape(rows, LANES), pltpu.HBM),
        pltpu.with_memory_space_constraint(momentum.reshape(block, LANES), pltpu.HBM),
    )
    full, moved = pl.pallas_call(
        put_out,
        out_shape=(
            jax.ShapeDtypeStruct((rows, LANES), f32),
            jax.ShapeDtypeStruct((block, LANES), f32),
        ),
        in_specs=[pl.BlockSpec(memory_space=pl.ANY)] * 2,
        out_specs=(hbm, hbm),
        scratch_shapes=[dma((2,))],
        compiler_params=pltpu.CompilerParams(vmem_limit_bytes=2**20),
        name="put_out",
    )(full, moved)
    return full.reshape(rows * LANES), moved.reshape(block * LANES)


def solution(mesh):
    return jax.shard_map(
        functools.partial(on_device, mesh.shape["rep"], mesh.shape["shard"]),
        mesh=mesh,
        in_specs=(P("rep", "shard"), P(), P("shard"), P(("shard", "rep"))),
        out_specs=(P("shard"), P(("shard", "rep"))),
        check_vma=False,
    )
```

time: 30.2 us -> 27.1 us (0.90)
  Pallas kernels: 29.5 us -> 26.3 us
    pallas_call x1, Pallas kernels: 28.4 us -> 25.2 us  [on_device(): pl.pallas_call(functools.partial(outer_step, replicas, shards, offsets.sh...]
where the time goes in v3:
time: 27.1 us; the launch traced here: 26.9 us
  Pallas kernels  26.3 us (97%)
  between operations  0.64 us (2%)
    pallas_call x1, Pallas kernels, on_device(): pl.pallas_call(functools.partial(outer_step, replicas, shards, offsets.sh...  25.2 us
    pallas_call x1, Pallas kernels, on_device(): pl.pallas_call(put_out, out_shape=(jax.ShapeDtypeStruct((rows, LANES), f3...  1.07 us

profile of v3, /device:TPU:0, one launch (start us, length us, event | category | flops | bytes accessed | tf_op | source)
XLA Modules:
  0.0 26.9 jit_solution(7673160560886668905)
XLA Ops:
  0.6 25.2 %outer_step.1 = (f32[2048,128]{1,0:T(8,128)S(1)}, f32[512,128]{1,0:T(8,128)S(1)}) custom-call(s32[65]{0:T(128)} %offsets.1, f32[2048,128]{1,0:T(8,128)} %bitcast.5, f32[2048,128]{1,0:T(8,128)} %bitcast.6, f32[512,128]{1,0:T(8,128)} %bitcast.7), custom_call_target="tpu_custom_call" | custom-call | tf_op jit(solution)/shard_map/outer_step/pallas_call | solution.py:295
  25.9 1.1 %put_out.1 = (f32[2048,128]{1,0:T(8,128)}, f32[512,128]{1,0:T(8,128)}) custom-call(f32[2048,128]{1,0:T(8,128)S(1)} %get-tuple-element.6.full, f32[512,128]{1,0:T(8,128)S(1)} %get-tuple-element.7.moved), custom_call_target="tpu_custom_call" | custom-call | tf_op jit(solution)/shard_map/put_out/pallas_call | solution.py:340

commit v4 on v3

--- a/solution.py
+++ b/solution.py
@@ -122,9 +122,15 @@
                 peer(step), mine, mine,
                 out_send.at[kind, step - 1, piece], out_recv.at[kind, step - 1, piece],
             )
-        own[kind, piece] = to(
-            twin, mine, mine, own_send.at[kind, piece], own_recv.at[kind, piece]
-        )
+        if kind == 2:
+            own[kind, piece] = to(
+                twin, mine, mine, own_send.at[kind, piece], own_recv.at[kind, piece]
+            )
+
+    def share_early(kind):
+        rows = pl.ds(pl.multiple_of(rep * block, 8), early * chunk)
+        mine = arrays[kind].at[rows]
+        own[kind, 0] = to(twin, mine, mine, own_send.at[kind, 0], own_recv.at[kind, 0])
 
     def pass_on(kind, piece):
         for step in peers:
@@ -204,15 +210,18 @@
         ).start()
         return carry
 
-    lax.fori_loop(1, devices, tell, 0)
+    lax.fori_loop(1, devices, tell, 0, unroll=devices <= 64)
 
     queue = []
     for piece in range(early):
         share(1, piece)
-        if (0, piece) not in own:
+        if piece > ahead:
             share(0, piece)
         queue.append((1, piece))
         queue.append((0, piece))
+    if early:
+        share_early(0)
+        share_early(1)
     queue.sort(key=lambda item: not (item[0] == 0 and item[1] <= ahead))
     for kind, piece in queue[:before]:
         pass_on(kind, piece)
@@ -238,9 +247,10 @@
         pass_on(kind, piece)
     for piece in range(early):
         new_momentum[part(piece)] = update(rep, piece)
-    for piece in range(early):
-        own[0, piece].wait_recv()
-        own[1, piece].wait_recv()
+    if early:
+        own[0, 0].wait_recv()
+        own[1, 0].wait_recv()
+    for piece in range(early):
         update(twin, piece)
     for piece in range(early):
         for step in peers:

time: 27.1 us -> 26.9 us (level)
  no operation moved by 1% of the time
where the time goes in v4:
time: 26.9 us; the launch traced here: 26.7 us
  Pallas kernels  26.1 us (97%)
  between operations  0.64 us (2%)
    pallas_call x1, Pallas kernels, on_device(): pl.pallas_call(functools.partial(outer_step, replicas, shards, offsets.sh...  25 us
    pallas_call x1, Pallas kernels, on_device(): pl.pallas_call(put_out, out_shape=(jax.ShapeDtypeStruct((rows, LANES), f3...  1.07 us

profile of v4, /device:TPU:0, one launch (start us, length us, event | category | flops | bytes accessed | tf_op | source)
XLA Modules:
  0.0 26.7 jit_solution(17896200228736152562)
XLA Ops:
  0.6 25.0 %outer_step.1 = (f32[2048,128]{1,0:T(8,128)S(1)}, f32[512,128]{1,0:T(8,128)S(1)}) custom-call(s32[65]{0:T(128)} %offsets.1, f32[2048,128]{1,0:T(8,128)} %bitcast.5, f32[2048,128]{1,0:T(8,128)} %bitcast.6, f32[512,128]{1,0:T(8,128)} %bitcast.7), custom_call_target="tpu_custom_call" | custom-call | tf_op jit(solution)/shard_map/outer_step/pallas_call | solution.py:305
  25.7 1.1 %put_out.1 = (f32[2048,128]{1,0:T(8,128)}, f32[512,128]{1,0:T(8,128)}) custom-call(f32[2048,128]{1,0:T(8,128)S(1)} %get-tuple-element.6.full, f32[512,128]{1,0:T(8,128)S(1)} %get-tuple-element.7.moved), custom_call_target="tpu_custom_call" | custom-call | tf_op jit(solution)/shard_map/put_out/pallas_call | solution.py:350
